TPU v7x, 32 devices: a whole 2x2x4 slice. The times are simulated.
32 devices in a mesh: tm: 4 (over y, x), chan: 8 (over z, core).
Axes of the slice: x: 2, y: 2, z: 4, core: 2. Of those that a mesh axis runs over, the one named last changes fastest.
Arguments:
- voltages: bfloat16 [8, 4, 32768, 512], P(None, None, ('tm', 'chan')), may hold values from -6 to 6
- taps: float32 [4, 512], replicated, may hold values from -3 to 3
- busy_mask: int32 [512], replicated, may hold values from 0 to 1, as said below
- drift_low: int32 [512], replicated, may hold values from -16 to 1
Outputs:
- drift_power: float32 [8, 32, 16, 2048], P(None, 'chan', None, 'tm')
Inputs may be any that keep to these rules, and one draw needn't show every extreme that they name: `busy_mask`: exactly 32 entries are 1.
All inputs are finite; a program needn't handle non-finite values.
Results may differ from a plain program's by a relative error of at most 0.008.
Values may be sent and summed in bfloat16 or wider, within the bound.
A program may use at most 192 MiB of HBM per device.

v0:
```python
import math

import jax
import jax.numpy as jnp
import numpy as np
from jax import lax
from jax.experimental import pallas as pl
from jax.experimental.pallas import tpu as pltpu
from jax.sharding import PartitionSpec as P

FA = 32
FB = 64
TAPS = 4
NDRIFT = 16
DSPAN = 16
FSTEP = 4
CH_DEV = 1


def passed_along(block, axis, distance):
    devices = range(lax.axis_size(axis))
    route = [(i - distance, i) for i in devices if i - distance in devices]
    return lax.ppermute(block, axis, route)


def busy_index(busy_mask, busy_count):
    before = jnp.cumsum(busy_mask) - busy_mask
    slot_ids = jnp.arange(busy_count, dtype=jnp.int32)
    is_slot = (busy_mask[:, None] == 1) & (before[:, None] == slot_ids[None, :])
    positions = jnp.arange(busy_mask.shape[0], dtype=jnp.int32)
    return jnp.sum(jnp.where(is_slot, positions[:, None], 0), axis=0)


def real_dft(sample_pos, freq_ids, length):
    phase_index = sample_pos[:, None] * freq_ids[None, :] % length
    angles = phase_index.astype(jnp.float32) * (2.0 * math.pi / length)
    cosines = jnp.cos(angles)
    sine_table = jnp.sin(angles)
    upper = jnp.stack([cosines, -sine_table], axis=1)
    lower = jnp.stack([sine_table, cosines], axis=1)
    return jnp.stack([upper, lower], axis=0).astype(jnp.bfloat16)


def to_bfloat(values):
    return lax.optimization_barrier(values.astype(jnp.bfloat16)).astype(jnp.float32)


def detect_power(spectra):
    items, lanes, chan_rows, samples = spectra.shape
    step_count = samples // (FA * FB)
    shaped = spectra.reshape(items, 2, 2, chan_rows, step_count, FA, FB)
    short_ids = jnp.arange(FA, dtype=jnp.int32)
    long_ids = jnp.arange(FB, dtype=jnp.int32)
    first_pass = jnp.einsum(
        "xopctab,paqf->xoqctfb",
        shaped,
        real_dft(short_ids, short_ids, FA),
        preferred_element_type=jnp.float32,
    )
    twist = short_ids[:, None] * long_ids[None, :] % (FA * FB)
    twist_angles = twist.astype(jnp.float32) * (2.0 * math.pi / (FA * FB))
    twist_cos = jnp.cos(twist_angles)
    twist_sin = jnp.sin(twist_angles)
    real_part = first_pass[:, :, 0]
    imag_part = first_pass[:, :, 1]
    turned = jnp.stack(
        [
            real_part * twist_cos + imag_part * twist_sin,
            imag_part * twist_cos - real_part * twist_sin,
        ],
        axis=2,
    ).astype(jnp.bfloat16)
    second_pass = jnp.einsum(
        "xoqctfb,qbsg->xosctgf",
        turned,
        real_dft(long_ids, long_ids, FB),
        preferred_element_type=jnp.float32,
    )
    powers = jnp.sum(second_pass * second_pass, axis=(1, 2)) / (4.0 * FA * FB)
    return powers.reshape(items, chan_rows, step_count, FA * FB)


def drift_rows(step_rows, first_step, drift_rates, first_bin, bin_width, pad_width):
    padded = jnp.pad(step_rows, ((0, 0), (0, 0), (0, 0), (pad_width, pad_width)))
    chan_rows = step_rows.shape[1]
    rate_count = drift_rates.shape[1]
    running = jnp.zeros((step_rows.shape[0], chan_rows, rate_count, bin_width), jnp.float32)
    for row_index in range(step_rows.shape[2]):
        step_time = first_step + row_index
        power_row = padded[:, 0, row_index]
        windows = []
        for rate_pos in range(rate_count):
            start = pad_width + first_bin + drift_rates[0, rate_pos] * step_time
            windows.append(lax.dynamic_slice_in_dim(power_row, start, bin_width, 1))
        per_slot = [jnp.stack(windows, axis=1)]
        running = running + jnp.stack(per_slot, axis=1)
    return running


def slot_rates(slot_part, drift_low):
    one_hot = slot_part[:, None] == jnp.arange(drift_low.shape[0], dtype=jnp.int32)[None, :]
    low_rates = jnp.sum(jnp.where(one_hot, drift_low[None, :], 0), axis=1)
    return low_rates[:, None] + jnp.arange(NDRIFT, dtype=jnp.int32)[None, :]


def shards(voltages, taps, busy_mask, drift_low):
    tm_count = lax.axis_size("tm")
    chan_devices = lax.axis_size("chan")
    count_of_beams, lanes, spec_dev, chan_count = voltages.shape
    busy_count = CH_DEV * tm_count * chan_devices
    step_count = FSTEP * tm_count
    pad_width = DSPAN * (step_count - 1)
    slot_index = busy_index(busy_mask, busy_count)
    slot_order = (
        slot_index.reshape(chan_devices, tm_count, CH_DEV).transpose(1, 0, 2).reshape(busy_count)
    )
    coarse_dft = real_dft(jnp.arange(chan_count, dtype=jnp.int32), slot_order, chan_count)
    following = passed_along(voltages[:, :, : TAPS - 1], ("tm", "chan"), -1)
    extended = jnp.concatenate([voltages, following], axis=2)
    filtered = taps[0] * extended[:, :, 0:spec_dev]
    for tap_index in range(1, TAPS):
        filtered = filtered + taps[tap_index] * extended[:, :, tap_index : tap_index + spec_dev]
    filtered = filtered.astype(jnp.bfloat16).reshape(count_of_beams, 2, 2, spec_dev, chan_count)
    coarse = jnp.einsum(
        "bopsn,pnqr->boqrs", filtered, coarse_dft, preferred_element_type=jnp.float32
    )
    coarse = (
        (coarse * chan_count ** (-0.5))
        .astype(jnp.bfloat16)
        .reshape(count_of_beams, 4, busy_count, spec_dev)
    )
    arrived = lax.all_to_all(
        lax.all_to_all(coarse, "tm", split_axis=2, concat_axis=3, tiled=True),
        "chan",
        split_axis=2,
        concat_axis=3,
        tiled=True,
    )
    ordered = arrived.reshape(count_of_beams, 4, CH_DEV, chan_devices, tm_count, spec_dev)
    ordered = ordered.transpose(0, 1, 2, 4, 3, 5).reshape(
        count_of_beams, 4, CH_DEV, tm_count * chan_devices * spec_dev
    )
    powers = detect_power(ordered)
    first_slot = lax.axis_index("chan") * (CH_DEV * tm_count) + lax.axis_index("tm") * CH_DEV
    drift_rates = slot_rates(lax.dynamic_slice_in_dim(slot_index, first_slot, CH_DEV), drift_low)
    drift_total = jnp.zeros((count_of_beams, CH_DEV, NDRIFT, FA * FB), jnp.float32)
    for group_index in range(tm_count):
        step_rows = powers[:, :, group_index * FSTEP : (group_index + 1) * FSTEP]
        drift_total = drift_total + to_bfloat(
            drift_rows(step_rows, group_index * FSTEP, drift_rates, 0, FA * FB, pad_width)
        )
    result = lax.all_to_all(
        (drift_total / step_count).astype(jnp.bfloat16),
        "tm",
        split_axis=3,
        concat_axis=1,
        tiled=True,
    ).astype(jnp.float32)
    return result


LANES = 128
FINE = FA * FB
SHORT = FINE // LANES
SLOTS = 32
HALO_ROWS = 8
PAD = 256


def tap_weights(taps, busy_mask):
    chan_count = busy_mask.shape[0]
    ids = np.arange(chan_count)
    angles = (ids[:, None] * ids[None, :] % chan_count) * (2.0 * math.pi / chan_count)
    cos_table = jnp.asarray(np.cos(angles), jnp.bfloat16)
    sin_table = jnp.asarray(np.sin(angles), jnp.bfloat16)
    earlier = jnp.asarray(ids[None, :] < ids[:, None])
    before = jnp.sum(jnp.where(earlier, busy_mask[None, :], 0), axis=1)
    column = np.arange(2 * LANES)
    slot = jnp.asarray(column % SLOTS, jnp.int32)
    picked = ((busy_mask[:, None] == 1) & (before[:, None] == slot[None, :])).astype(jnp.bfloat16)
    cosines = jnp.dot(cos_table, picked, preferred_element_type=jnp.float32)
    sines = jnp.dot(sin_table, picked, preferred_element_type=jnp.float32)
    imag = jnp.asarray(column // 64 % 2 == 1)[None, :]
    upper = jnp.where(imag, -sines, cosines)
    lower = jnp.where(imag, cosines, sines)
    scaled = (taps * chan_count ** (-0.5)).T
    weights = []
    for pol in range(2):
        tap_of = 2 * (column // LANES) + (column // SLOTS % 2 ^ pol)
        factor = jnp.zeros((chan_count, 2 * LANES), jnp.float32)
        for tap in range(TAPS):
            factor = jnp.where(jnp.asarray(tap_of == tap)[None, :], scaled[:, tap : tap + 1], factor)
        weights += [(upper * factor).astype(jnp.bfloat16), (lower * factor).astype(jnp.bfloat16)]
    slot_low = lambda drift_low: jnp.sum(
        jnp.where(picked[:, :SLOTS] == 1, drift_low[:, None], 0), axis=0
    )
    return weights, slot_low


def coarse_kernel(first_ref, volt_ref, halo_ref, w00, w01, w10, w11, out_ref, g00, g01, g10, g11):
    rows = volt_ref.shape[2]
    chunk = min(rows, 256)
    for pol, (wa, wb, left, right) in enumerate(((w00, w01, g00, g01), (w10, w11, g10, g11))):
        for start in range(0, rows, chunk):
            part = jnp.dot(
                volt_ref[0, 2 * pol, start : start + chunk], wa[...], preferred_element_type=jnp.float32
            ) + jnp.dot(
                volt_ref[0, 2 * pol + 1, start : start + chunk], wb[...], preferred_element_type=jnp.float32
            )
            left[start : start + chunk] = part[:, :LANES]
            right[start : start + chunk] = part[:, LANES:]
        part = jnp.dot(
            halo_ref[0, 2 * pol], wa[...], preferred_element_type=jnp.float32
        ) + jnp.dot(halo_ref[0, 2 * pol + 1], wb[...], preferred_element_type=jnp.float32)
        left[rows : rows + HALO_ROWS] = part[:, :LANES]
        right[rows : rows + HALO_ROWS] = part[:, LANES:]
    count = rows // SHORT
    first_pol = lax.broadcasted_iota(jnp.int32, (count, LANES), 1) // SLOTS % 2 == 0

    def both(at):
        low = pl.ds(at, count, stride=SHORT)
        high = pl.ds(at + 2, count, stride=SHORT)
        return g00[low, :] + g01[high, :], g10[low, :] + g11[high, :]

    here = both(0)
    for at in range(SHORT):
        after = both(at + 1)
        value = jnp.where(
            first_pol,
            here[0] + pltpu.roll(after[0], LANES - SLOTS, 1),
            here[1] + pltpu.roll(after[1], SLOTS, 1),
        )
        out_ref[0, at * count : (at + 1) * count, :] = value.astype(jnp.bfloat16)
        here = after


def coarse_items(voltages, halo, weights, first, items):
    beams, lanes, rows, chan_count = voltages.shape
    whole = pl.BlockSpec((chan_count, 2 * LANES), lambda i, s: (0, 0))
    return pl.pallas_call(
        coarse_kernel,
        grid_spec=pltpu.PrefetchScalarGridSpec(
            num_scalar_prefetch=1,
            grid=(items,),
            in_specs=[
                pl.BlockSpec((1, lanes, rows, chan_count), lambda i, s: (s[0] + i, 0, 0, 0)),
                pl.BlockSpec((1, lanes, HALO_ROWS, chan_count), lambda i, s: (s[0] + i, 0, 0, 0)),
                whole,
                whole,
                whole,
                whole,
            ],
            out_specs=pl.BlockSpec((1, rows, LANES), lambda i, s: (i, 0, 0)),
            scratch_shapes=[pltpu.VMEM((rows + 3 * HALO_ROWS, LANES), jnp.float32)] * 4,
        ),
        out_shape=jax.ShapeDtypeStruct((items, rows, LANES), jnp.bfloat16),
        compiler_params=pltpu.CompilerParams(vmem_limit_bytes=48 * 2**20),
        cost_estimate=pl.CostEstimate(
            flops=items * lanes * rows * chan_count * 4 * LANES,
            bytes_accessed=items * lanes * rows * chan_count * 2,
            transcendentals=0,
        ),
    )(first.reshape(1), voltages, halo, *weights)


def short_dft(values, sign):
    count = len(values)
    if count == 1:
        return values
    even = short_dft(values[0::2], sign)
    odd = short_dft(values[1::2], sign)
    low, high = [], []
    for k in range(count // 2):
        term = odd[k]
        if k:
            flipped = pltpu.roll(term, LANES // 2, 1)
            angle = 2.0 * math.pi * k / count
            if 4 * k == count:
                term = flipped * sign
            else:
                term = term * math.cos(angle) + flipped * (sign * math.sin(angle))
        low.append(even[k] + term)
        high.append(even[k] - term)
    return low + high


def fine_kernel(core_ref, own_ref, other_ref, dft_ref, pick_ref, out_ref, mid, power):
    items, rows, _ = own_ref.shape
    count = rows // SHORT
    is_first = core_ref[0] == 0
    sign_of = lambda n: jnp.where(
        lax.broadcasted_iota(jnp.int32, (n, LANES), 1) < LANES // 2, 1.0, -1.0
    ).astype(jnp.float32)
    sign_full = sign_of(2 * count)
    for at in range(SHORT):
        plain, flipped = [], []
        for item in range(items):
            own = own_ref[item, at * count : (at + 1) * count, :]
            other = other_ref[item, at * count : (at + 1) * count, :]
            block = jnp.concatenate(
                [jnp.where(is_first, own, other), jnp.where(is_first, other, own)], axis=0
            )
            plain.append(block)
            swapped = pltpu.roll(block.astype(jnp.float32), LANES // 2, 1) * sign_full
            flipped.append(swapped.astype(jnp.bfloat16))
        stacked = jnp.concatenate(
            [jnp.concatenate(plain, axis=1), jnp.concatenate(flipped, axis=1)], axis=0
        )
        mid[at] = jnp.dot(dft_ref[at], stacked, preferred_element_type=jnp.float32)
    step = 16
    sign = sign_of(step)
    for item in range(items):
        lanes = pl.ds(item * LANES, LANES)

        @pl.loop(0, LANES // step)
        def _(block):
            at_row = pl.multiple_of(block * step, step)
            spectra = short_dft([mid[at, pl.ds(at_row, step), lanes] for at in range(SHORT)], sign)
            for high, value in enumerate(spectra):
                where = pl.ds(pl.multiple_of(high * LANES + at_row, step), step)
                power[where, lanes] = (value * value).astype(jnp.bfloat16)

    width = 512
    for start in range(0, SHORT * LANES, width):
        out_ref[:, start : start + width] = lax.dot_general(
            pick_ref[...],
            power[start : start + width, :],
            (((1,), (1,)), ((), ())),
            preferred_element_type=jnp.float32,
        ).astype(jnp.bfloat16)


def fine_powers(own, other, core, groups):
    items, rows, _ = own.shape
    position = np.arange(SHORT)[:, None, None] + SHORT * np.arange(LANES)[None, None, :]
    angles = (position * np.arange(LANES)[None, :, None] % FINE) * (2.0 * math.pi / FINE)
    dft = jnp.asarray(np.concatenate([np.cos(angles), np.sin(angles)], axis=2), jnp.bfloat16)
    per_group = SLOTS // groups
    row = np.arange(SLOTS * items)
    row_group, row_slot, row_item = row // (per_group * items), row // items % per_group, row % items
    lane = np.arange(items * LANES)
    pick = (row_item[:, None] == lane[None, :] // LANES) & (
        (row_group * per_group + row_slot)[:, None] == lane[None, :] % SLOTS
    )
    vmem = pl.BlockSpec(memory_space=pltpu.VMEM)
    return pl.pallas_call(
        fine_kernel,
        in_specs=[pl.BlockSpec(memory_space=pltpu.SMEM), vmem, vmem, vmem, vmem],
        out_specs=vmem,
        out_shape=jax.ShapeDtypeStruct((SLOTS * items, FINE), jnp.bfloat16),
        scratch_shapes=[
            pltpu.VMEM((SHORT, LANES, items * LANES), jnp.float32),
            pltpu.VMEM((FINE, items * LANES), jnp.bfloat16),
        ],
        compiler_params=pltpu.CompilerParams(vmem_limit_bytes=48 * 2**20),
        cost_estimate=pl.CostEstimate(flops=2 * 10**9, bytes_accessed=4 * 10**6, transcendentals=0),
    )(core.reshape(1), own, other, dft, jnp.asarray(pick, jnp.bfloat16))


def window_start(part, width):
    return jnp.clip(part * width - PAD, 0, FINE - (width + 2 * PAD))


def exchange_kernel(tm_count, chan_devices, in_ref, out_ref, held, sent1, came1, sent2, came2, local):
    tm, chan = lax.axis_index("tm"), lax.axis_index("chan")
    window = out_ref.shape[3]
    width = FINE // tm_count
    MESH = pl.DeviceIdType.MESH
    tm_peers = [lax.rem(tm + q, tm_count) for q in range(tm_count)]
    chan_peers = [lax.rem(chan + k, chan_devices) for k in range(chan_devices)]
    chan_from = [lax.rem(chan + chan_devices - k, chan_devices) for k in range(chan_devices)]
    tm_from = [lax.rem(tm + tm_count - q, tm_count) for q in range(tm_count)]
    barrier = pltpu.get_barrier_semaphore()
    for q in range(1, tm_count):
        pl.semaphore_signal(barrier, inc=1, device_id=(tm_peers[q], chan), device_id_type=MESH)
    for k in range(1, chan_devices):
        pl.semaphore_signal(barrier, inc=1, device_id=(tm, chan_peers[k]), device_id_type=MESH)
    pl.semaphore_wait(barrier, tm_count + chan_devices - 2)

    first = []
    for k in range(1, chan_devices):
        copy = pltpu.make_async_remote_copy(
            src_ref=in_ref.at[chan_peers[k]],
            dst_ref=held.at[k],
            send_sem=sent1.at[k],
            recv_sem=came1.at[k],
            device_id=(tm, chan_peers[k]),
            device_id_type=MESH,
        )
        copy.start()
        first.append(copy)
    second, near = [], []
    for k in range(chan_devices):
        if k:
            first[k - 1].wait_recv()
        block = held.at[k] if k else in_ref.at[chan]
        for q in range(1, tm_count):
            start = pl.multiple_of(window_start(tm_peers[q], width), LANES)
            copy = pltpu.make_async_remote_copy(
                src_ref=block.at[:, pl.ds(start, window)],
                dst_ref=out_ref.at[tm, chan_from[k]],
                send_sem=sent2.at[k, q],
                recv_sem=came2.at[k, q],
                device_id=(tm_peers[q], chan),
                device_id_type=MESH,
            )
            copy.start()
            second.append(copy)
        start = pl.multiple_of(window_start(tm, width), LANES)
        copy = pltpu.make_async_copy(
            block.at[:, pl.ds(start, window)], out_ref.at[tm, chan_from[k]], local.at[k]
        )
        copy.start()
        near.append(copy)
    for copy in first + second:
        copy.wait_send()
    for copy in near:
        copy.wait()
    for k in range(chan_devices):
        for q in range(1, tm_count):
            pltpu.make_async_remote_copy(
                src_ref=held.at[k, :, pl.ds(0, window)],
                dst_ref=out_ref.at[tm_from[q], chan_from[k]],
                send_sem=sent2.at[k, q],
                recv_sem=came2.at[k, q],
                device_id=(tm_peers[q], chan),
                device_id_type=MESH,
            ).wait_recv()


def exchange(powers, tm_count, chan_devices):
    rows = powers.shape[1]
    window = FINE // tm_count + 2 * PAD
    vmem = pl.BlockSpec(memory_space=pltpu.VMEM)
    kernel = lambda *refs: exchange_kernel(tm_count, chan_devices, *refs)
    dma = pltpu.SemaphoreType.DMA
    return pl.pallas_call(
        kernel,
        in_specs=[vmem],
        out_specs=vmem,
        out_shape=jax.ShapeDtypeStruct((tm_count, chan_devices, rows, window), jnp.bfloat16),
        scratch_shapes=[
            pltpu.VMEM(powers.shape, jnp.bfloat16),
            dma((chan_devices,)),
            dma((chan_devices,)),
            dma((chan_devices, tm_count)),
            dma((chan_devices, tm_count)),
            dma((chan_devices,)),
        ],
        compiler_params=pltpu.CompilerParams(collective_id=0, has_side_effects=True),
    )(powers)


def drift_kernel(scale, low_ref, in_ref, out_ref, rows_ref):
    steps, cores, _, window = in_ref.shape
    beams, slots, rates, width = out_ref.shape
    items = beams // cores
    edge = jnp.zeros(rows_ref.shape[:3] + (PAD,), jnp.float32)
    rows_ref[:, :, :, :PAD] = edge
    rows_ref[:, :, :, PAD + window :] = edge
    offset = low_ref[slots]
    for t in range(steps):
        halves = [in_ref[t, core].astype(jnp.float32) for core in range(cores)]
        for slot in range(slots):
            rows_ref[slot, t, :, PAD : PAD + window] = jnp.concatenate(
                [half[slot * items : (slot + 1) * items] for half in halves], axis=0
            )
    lane = lax.broadcasted_iota(jnp.int32, (beams, LANES), 1)
    tiles = width // LANES
    for slot in range(slots):
        low = low_ref[slot]
        for rate in range(rates):
            totals = [jnp.zeros((beams, LANES), jnp.float32)] * tiles
            for t in range(steps):
                start = (low + rate) * t + PAD + offset
                rest = lax.rem(start, LANES)
                base = start - rest
                turned = []
                for tile in range(tiles + 1):
                    at = pl.ds(pl.multiple_of(base + tile * LANES, LANES), LANES)
                    turned.append(rows_ref[slot, t, :, at])
                if t:
                    back = LANES - rest
                    turned = [pltpu.roll(part, back, 1) for part in turned]
                    keep = lane < back
                    turned = [jnp.where(keep, turned[k], turned[k + 1]) for k in range(tiles)]
                totals = [total + part for total, part in zip(totals, turned)]
            out_ref[:, slot, rate, :] = jnp.concatenate(totals, axis=1) * scale


def drift_sums(rows, low_rates, offset, beams, width):
    steps = rows.shape[0]
    slots = low_rates.shape[0]
    vmem = pl.BlockSpec(memory_space=pltpu.VMEM)
    kernel = lambda *refs: drift_kernel(1.0 / (4.0 * FINE * steps), *refs)
    return pl.pallas_call(
        kernel,
        in_specs=[pl.BlockSpec(memory_space=pltpu.SMEM), vmem],
        out_specs=vmem,
        out_shape=jax.ShapeDtypeStruct((beams, slots, NDRIFT, width), jnp.float32),
        scratch_shapes=[pltpu.VMEM((slots, steps, beams, rows.shape[3] + 2 * PAD), jnp.float32)],
        compiler_params=pltpu.CompilerParams(vmem_limit_bytes=48 * 2**20),
    )(jnp.concatenate([low_rates, offset[None]]), rows)


def paired_shards(voltages, taps, busy_mask, drift_low):
    tm_count = lax.axis_size("tm")
    chan_devices = lax.axis_size("chan")
    beams, lanes, rows, chan_count = voltages.shape
    items = beams // 2
    slots = SLOTS // chan_devices
    chan = lax.axis_index("chan")
    core = lax.rem(chan, 2)
    halo = passed_along(voltages[:, :, :HALO_ROWS], ("tm", "chan"), -1)
    weights, slot_low = tap_weights(taps, busy_mask)
    low_rates = lax.dynamic_slice_in_dim(slot_low(drift_low), chan * slots, slots)
    sent = coarse_items(voltages, halo, weights, (1 - core) * items, items)
    other = lax.ppermute(sent, "chan", [(i, i ^ 1) for i in range(chan_devices)])
    own = coarse_items(voltages, halo, weights, core * items, items)
    powers = fine_powers(own, other, core, chan_devices)
    powers = powers.reshape(chan_devices, slots * items, FINE)
    width = FINE // tm_count
    arrived = exchange(powers, tm_count, chan_devices).reshape(
        tm_count * chan_devices // 2, 2, slots * items, width + 2 * PAD
    )
    tm = lax.axis_index("tm")
    offset = tm * width - window_start(tm, width)
    return drift_sums(arrived, low_rates, offset, beams, width)


def two_devices_hold_a_step(mesh, voltages):
    tm_count, chan_devices = mesh.shape["tm"], mesh.shape["chan"]
    rows = voltages.shape[2] // (tm_count * chan_devices)
    return (
        2 * rows == FINE
        and chan_devices == 2 * FSTEP
        and CH_DEV * tm_count * chan_devices == SLOTS
        and voltages.shape[0] == 8
        and PAD >= DSPAN * (FSTEP * tm_count - 1)
        and FINE // tm_count % PAD == 0
        and FINE // tm_count + 2 * PAD <= FINE
    )


def solution(mesh):
    in_specs = (P(None, None, ("tm", "chan"), None), P(), P(), P())
    out_specs = P(None, "chan", None, "tm")

    def run(voltages, taps, busy_mask, drift_low):
        body = paired_shards if two_devices_hold_a_step(mesh, voltages) else shards
        return jax.shard_map(
            body, mesh=mesh, in_specs=in_specs, out_specs=out_specs, check_vma=False
        )(voltages, taps, busy_mask, drift_low)

    return run
```

profile of v0, /device:TPU:0, one launch (start us, length us, event | category | flops | bytes accessed | tf_op | source)
XLA Modules:
  0.0 79.7 jit_solution(6358851965935983067)
XLA Ops:
  0.0 0.0 copy-start.4
  0.0 0.0 copy-start.5
  0.0 1.0 %slice.27 = bf16[8,4,8,512]{3,2,1,0:T(8,128)(2,1)S(1)} slice(bf16[8,4,1024,512]{3,2,1,0:T(8,128)(2,1)} %volt_ref.3), slice={[0:8], [0:4], [0:8], [0:512]} | slice | bytes 524288 | tf_op jit(solution)/shard_map/slice | solution.py:514
  1.0 1.3 %collective-permute-start = (bf16[8,4,8,512]{3,2,1,0:T(8,128)(2,1)S(1)}, bf16[8,4,8,512]{3,2,1,0:T(8,128)(2,1)S(1)}, u32[]{:S(2)}, u32[]{:S(2)}) collective-permute-start(bf16[8,4,8,512]{3,2,1,0:T(8,128)(2,1)S(1)} %slice.27), channel_id=1, source_target_pairs={{1,0},{2,1},{3,2},{4,3},{5,4},{6,5},{7,6},{8,7},{9,8},{10,9},{11,1... | collective-permute-start | bytes 786440 | tf_op jit(solution)/shard_map/ppermute | solution.py:23
  2.3 0.7 broadcast_compare_fusion
  3.0 1.2 %select_reduce_fusion = s32[512]{0:T(512)S(1)} fusion(pred[512,512]{1,0:T(32,128)(4,1)} %constant.57.clone, s32[512]{0:T(512)} %param.21), kind=kLoop, calls=%fused_computation | loop fusion | flops 523776 | bytes 266240 | tf_op jit(solution)/shard_map/reduce_sum | solution.py:177
  4.2 0.7 multiply_bitcast_fusion
  4.9 1.5 %fusion.1 = f32[512,256]{1,0:T(8,128)S(1)} fusion(bf16[512,512]{1,0:T(8,128)(2,1)} %constant.56.clone, s32[512]{0:T(512)S(1)} %select_reduce_fusion, s32[256]{0:T(256)} %constant.58.clone, pred[512]{0:T(512)(128)(4,1)S(1)} %broadcast_compare_fusion), kind=kOutput, calls=%fused_computation.16 | convolution fusion | flops 134479872 | bytes 1052160 | tf_op jit(solution)/shard_map/dot_general | solution.py:182
  6.4 1.7 %multiply_convert_fusion = (bf16[512,256]{1,0:T(8,128)(2,1)S(1)}, bf16[512,256]{1,0:T(8,128)(2,1)S(1)}, bf16[512,256]{1,0:T(8,128)(2,1)S(1)}, bf16[512,256]{1,0:T(8,128)(2,1)S(1)}) fusion(f32[512]{0:T(512)S(1)} %bitcast.17, f32[512]{0:T(512)S(1)} %bitcast.18, f32[512]{0:T(512)S(1)} %bitcast.19, f32[512]{0:T(512)S(1)} %bitcast.16, ...), kind=kOutput, calls=%fused_computation.1 | convolution fusion | flops 136970240 | bytes 2110208 | tf_op jit(solution)/shard_map/dot_general | solution.py:181
  8.0 0.0 collective-permute-done.halo_ref
  8.0 0.0 copy-start.3
  8.0 9.8 %shard_map.182 = bf16[4,1024,128]{2,1,0:T(8,128)(2,1)S(1)} custom-call(s32[1]{0:T(128)} %bitcast.8.first_ref, bf16[8,4,1024,512]{3,2,1,0:T(8,128)(2,1)} %volt_ref.3, bf16[8,4,8,512]{3,2,1,0:T(8,128)(2,1)S(1)} %collective-permute-done.halo_ref, bf16[512,256]{1,0:T(8,128)(2,1)S(1)} %get-tuple-element.8.w00, bf16[512,256]{1,0:T(8,128)(2,1)S(1)} %get-tuple-element.7.w01, ...), custom_call_target="tpu_custom_call" | custom-call | flops 4294967296 | bytes 16777216 | tf_op jit(solution)/shard_map/pallas_call | solution.py:240
  17.9 2.1 %collective-permute-start.1 = (bf16[4,1024,128]{2,1,0:T(8,128)(2,1)S(1)}, bf16[4,1024,128]{2,1,0:T(8,128)(2,1)S(1)}, u32[]{:S(2)}, u32[]{:S(2)}) collective-permute-start(bf16[4,1024,128]{2,1,0:T(8,128)(2,1)S(1)} %shard_map.182), channel_id=1, source_target_pairs={{0,1},{1,0},{2,3},{3,2},{4,5},{5,4},{6,7},{7,6},{8,9},{9,8},{10,11... | collective-permute-start | bytes 3145736 | tf_op jit(solution)/shard_map/ppermute | solution.py:518
  20.0 0.0 copy-done.4
  20.0 0.0 copy-start.2
  20.0 0.2 compare_and_fusion
  20.2 0.0 copy-done.5
  20.2 0.1 select_reduce_fusion.1
  20.3 0.1 dynamic_slice.3
  20.4 0.1 pad_add_fusion.refs_0_
  20.5 9.8 %shard_map.181.own_ref = bf16[4,1024,128]{2,1,0:T(8,128)(2,1)S(1)} custom-call(s32[1]{0:T(128)} %bitcast.2.first_ref, bf16[8,4,1024,512]{3,2,1,0:T(8,128)(2,1)} %volt_ref.3, bf16[8,4,8,512]{3,2,1,0:T(8,128)(2,1)S(1)} %collective-permute-done.halo_ref, bf16[512,256]{1,0:T(8,128)(2,1)S(1)} %get-tuple-element.8.w00, bf16[512,256]{1,0:T(8,128)(2,1)S(1)} %get-tuple-element.7.w01, ...), custom_call_target="tpu_custom_call" | custom-call | flops 4294967296 | bytes 16777216 | tf_op jit(solution)/shard_map/pallas_call | solution.py:240
  30.3 0.0 collective-permute-done.1.other_ref
  30.3 0.0 copy-done.3
  30.3 0.0 copy-done.2
  30.3 9.4 %shard_map.183 = bf16[128,2048]{1,0:T(8,128)(2,1)S(1)} custom-call(s32[1]{0:T(128)} %bitcast.1.core_ref, bf16[4,1024,128]{2,1,0:T(8,128)(2,1)S(1)} %shard_map.181.own_ref, bf16[4,1024,128]{2,1,0:T(8,128)(2,1)S(1)} %collective-permute-done.1.other_ref, bf16[16,128,256]{2,1,0:T(8,128)(2,1)S(1)} %copy-done.2, bf16[128,512]{1,0:T(8,128)(2,1)S(1)} %copy-done.3), custom_call_target="tpu_custom_call" | custom-call | flops 2000000000 | bytes 4000000 | tf_op jit(solution)/shard_map/pallas_call | solution.py:346
  39.8 0.0 copy-start.1
  39.8 0.8 copy-done.1
  40.6 27.6 %shard_map.184 = bf16[4,8,16,1024]{3,2,1,0:T(8,128)(2,1)} custom-call(bf16[8,16,2048]{2,1,0:T(8,128)(2,1)} %bitcast.15), custom_call_target="tpu_custom_call" | custom-call | tf_op jit(solution)/shard_map/pallas_call | solution.py:437
  68.1 0.0 copy-start
  68.1 1.2 %copy-done = bf16[4,8,16,1024]{3,2,1,0:T(8,128)(2,1)S(1)} copy-done((bf16[4,8,16,1024]{3,2,1,0:T(8,128)(2,1)S(1)}, bf16[4,8,16,1024]{3,2,1,0:T(8,128)(2,1)}, u32[]{:S(2)}) %copy-start) | copy-done | bytes 1048600
  69.4 10.4 %shard_map.185 = f32[8,4,16,512]{3,2,1,0:T(8,128)} custom-call(s32[5]{0:T(128)S(1)} %pad_add_fusion.refs_0_, bf16[16,2,16,1024]{3,2,1,0:T(8,128)(2,1)S(1)} %bitcast.14), custom_call_target="tpu_custom_call" | custom-call | tf_op jit(solution)/shard_map/pallas_call | solution.py:496
  (1 shorter events, 0.0 us)
Async XLA Ops:
  0.0 20.0 %copy-start.4 = (s32[256]{0:T(256)S(1)}, s32[256]{0:T(256)}, u32[]{:S(2)}) copy-start(s32[256]{0:T(256)} %constant.58.clone) | copy-start | bytes 3076
  0.0 20.2 %copy-start.5 = (s32[512]{0:T(512)S(1)}, s32[512]{0:T(512)}, u32[]{:S(2)}) copy-start(s32[512]{0:T(512)} %param.22) | copy-start | bytes 6148
  1.0 7.0 %collective-permute-start = (bf16[8,4,8,512]{3,2,1,0:T(8,128)(2,1)S(1)}, bf16[8,4,8,512]{3,2,1,0:T(8,128)(2,1)S(1)}, u32[]{:S(2)}, u32[]{:S(2)}) collective-permute-start(bf16[8,4,8,512]{3,2,1,0:T(8,128)(2,1)S(1)} %slice.27), channel_id=1, source_target_pairs={{1,0},{2,1},{3,2},{4,3},{5,4},{6,5},{7,6},{8,7},{9,8},{10,9},{11,1... | collective-permute-start | bytes 786440 | tf_op jit(solution)/shard_map/ppermute | solution.py:23
  8.0 22.3 %copy-start.3 = (bf16[128,512]{1,0:T(8,128)(2,1)S(1)}, bf16[128,512]{1,0:T(8,128)(2,1)}, u32[]{:S(2)}) copy-start(bf16[128,512]{1,0:T(8,128)(2,1)} %constant.65.clone.pick_ref) | copy-start | bytes 393220
  17.9 12.4 %collective-permute-start.1 = (bf16[4,1024,128]{2,1,0:T(8,128)(2,1)S(1)}, bf16[4,1024,128]{2,1,0:T(8,128)(2,1)S(1)}, u32[]{:S(2)}, u32[]{:S(2)}) collective-permute-start(bf16[4,1024,128]{2,1,0:T(8,128)(2,1)S(1)} %shard_map.182), channel_id=1, source_target_pairs={{0,1},{1,0},{2,3},{3,2},{4,5},{5,4},{6,7},{7,6},{8,9},{9,8},{10,11... | collective-permute-start | bytes 3145736 | tf_op jit(solution)/shard_map/ppermute | solution.py:518
  20.0 10.3 %copy-start.2 = (bf16[16,128,256]{2,1,0:T(8,128)(2,1)S(1)}, bf16[16,128,256]{2,1,0:T(8,128)(2,1)}, u32[]{:S(2)}) copy-start(bf16[16,128,256]{2,1,0:T(8,128)(2,1)} %constant.64.clone.dft_ref) | copy-start | bytes 3145732
  39.8 0.8 copy-start.1
  68.1 1.2 %copy-start = (bf16[4,8,16,1024]{3,2,1,0:T(8,128)(2,1)S(1)}, bf16[4,8,16,1024]{3,2,1,0:T(8,128)(2,1)}, u32[]{:S(2)}) copy-start(bf16[4,8,16,1024]{3,2,1,0:T(8,128)(2,1)} %shard_map.184) | copy-start | bytes 3145732
where the time goes:
time: 80.2 us; the launch traced here: 79.7 us
  Pallas kernels  67 us (84%)
  starting transfers between devices  3.43 us (4%)
  matrix products  3.13 us (4%)
  local copies, waits for them, and re-layouts  3.1 us (4%)
  other arithmetic  2.9 us (4%)
    pallas_call x1, Pallas kernels, exchange(): pl.pallas_call(kernel, in_specs=[vmem], out_specs=vmem, out_shape=jax.Sha...  27.6 us
    pallas_call x2, Pallas kernels, coarse_items(): pl.pallas_call(coarse_kernel, grid_spec=pltpu.PrefetchScalarGridSpec(num_...  19.7 us
    pallas_call x1, Pallas kernels, drift_sums(): pl.pallas_call(kernel, in_specs=[pl.BlockSpec(memory_space=pltpu.SMEM), v...  10.4 us
    pallas_call x1, Pallas kernels, fine_powers(): pl.pallas_call(fine_kernel, in_specs=[pl.BlockSpec(memory_space=pltpu.SME...  9.41 us
    ppermute x1, starting transfers between devices, paired_shards(): lax.ppermute(sent, 'chan', [(i, i ^ 1) for i in range(chan_devices)])  2.14 us
    unnamed x12, local copies, waits for them, and re-layouts  2.02 us
    dot_general x1, matrix products, tap_weights(): cosines = jnp.dot(cos_table, picked, preferred_element_type=jnp.float32)  1.65 us
  transfers between devices with their start and end apart: 2, of which 0 were waited for; matrix products, arithmetic and copies ran while one was open for 8% of the time, Pallas kernels for 12%

commit v1 on v0

v1 whole, which is shorter than its diff:
```python
import math

import jax
import jax.numpy as jnp
import numpy as np
from jax import lax
from jax.experimental import pallas as pl
from jax.experimental.pallas import tpu as pltpu
from jax.sharding import PartitionSpec as P

FA = 32
FB = 64
TAPS = 4
NDRIFT = 16
DSPAN = 16
FSTEP = 4
CH_DEV = 1


def passed_along(block, axis, distance):
    devices = range(lax.axis_size(axis))
    route = [(i - distance, i) for i in devices if i - distance in devices]
    return lax.ppermute(block, axis, route)


def busy_index(busy_mask, busy_count):
    before = jnp.cumsum(busy_mask) - busy_mask
    slot_ids = jnp.arange(busy_count, dtype=jnp.int32)
    is_slot = (busy_mask[:, None] == 1) & (before[:, None] == slot_ids[None, :])
    positions = jnp.arange(busy_mask.shape[0], dtype=jnp.int32)
    return jnp.sum(jnp.where(is_slot, positions[:, None], 0), axis=0)


def real_dft(sample_pos, freq_ids, length):
    phase_index = sample_pos[:, None] * freq_ids[None, :] % length
    angles = phase_index.astype(jnp.float32) * (2.0 * math.pi / length)
    cosines = jnp.cos(angles)
    sine_table = jnp.sin(angles)
    upper = jnp.stack([cosines, -sine_table], axis=1)
    lower = jnp.stack([sine_table, cosines], axis=1)
    return jnp.stack([upper, lower], axis=0).astype(jnp.bfloat16)


def to_bfloat(values):
    return lax.optimization_barrier(values.astype(jnp.bfloat16)).astype(jnp.float32)


def detect_power(spectra):
    items, lanes, chan_rows, samples = spectra.shape
    step_count = samples // (FA * FB)
    shaped = spectra.reshape(items, 2, 2, chan_rows, step_count, FA, FB)
    short_ids = jnp.arange(FA, dtype=jnp.int32)
    long_ids = jnp.arange(FB, dtype=jnp.int32)
    first_pass = jnp.einsum(
        "xopctab,paqf->xoqctfb",
        shaped,
        real_dft(short_ids, short_ids, FA),
        preferred_element_type=jnp.float32,
    )
    twist = short_ids[:, None] * long_ids[None, :] % (FA * FB)
    twist_angles = twist.astype(jnp.float32) * (2.0 * math.pi / (FA * FB))
    twist_cos = jnp.cos(twist_angles)
    twist_sin = jnp.sin(twist_angles)
    real_part = first_pass[:, :, 0]
    imag_part = first_pass[:, :, 1]
    turned = jnp.stack(
        [
            real_part * twist_cos + imag_part * twist_sin,
            imag_part * twist_cos - real_part * twist_sin,
        ],
        axis=2,
    ).astype(jnp.bfloat16)
    second_pass = jnp.einsum(
        "xoqctfb,qbsg->xosctgf",
        turned,
        real_dft(long_ids, long_ids, FB),
        preferred_element_type=jnp.float32,
    )
    powers = jnp.sum(second_pass * second_pass, axis=(1, 2)) / (4.0 * FA * FB)
    return powers.reshape(items, chan_rows, step_count, FA * FB)


def drift_rows(step_rows, first_step, drift_rates, first_bin, bin_width, pad_width):
    padded = jnp.pad(step_rows, ((0, 0), (0, 0), (0, 0), (pad_width, pad_width)))
    chan_rows = step_rows.shape[1]
    rate_count = drift_rates.shape[1]
    running = jnp.zeros((step_rows.shape[0], chan_rows, rate_count, bin_width), jnp.float32)
    for row_index in range(step_rows.shape[2]):
        step_time = first_step + row_index
        power_row = padded[:, 0, row_index]
        windows = []
        for rate_pos in range(rate_count):
            start = pad_width + first_bin + drift_rates[0, rate_pos] * step_time
            windows.append(lax.dynamic_slice_in_dim(power_row, start, bin_width, 1))
        per_slot = [jnp.stack(windows, axis=1)]
        running = running + jnp.stack(per_slot, axis=1)
    return running


def slot_rates(slot_part, drift_low):
    one_hot = slot_part[:, None] == jnp.arange(drift_low.shape[0], dtype=jnp.int32)[None, :]
    low_rates = jnp.sum(jnp.where(one_hot, drift_low[None, :], 0), axis=1)
    return low_rates[:, None] + jnp.arange(NDRIFT, dtype=jnp.int32)[None, :]


def shards(voltages, taps, busy_mask, drift_low):
    tm_count = lax.axis_size("tm")
    chan_devices = lax.axis_size("chan")
    count_of_beams, lanes, spec_dev, chan_count = voltages.shape
    busy_count = CH_DEV * tm_count * chan_devices
    step_count = FSTEP * tm_count
    pad_width = DSPAN * (step_count - 1)
    slot_index = busy_index(busy_mask, busy_count)
    slot_order = (
        slot_index.reshape(chan_devices, tm_count, CH_DEV).transpose(1, 0, 2).reshape(busy_count)
    )
    coarse_dft = real_dft(jnp.arange(chan_count, dtype=jnp.int32), slot_order, chan_count)
    following = passed_along(voltages[:, :, : TAPS - 1], ("tm", "chan"), -1)
    extended = jnp.concatenate([voltages, following], axis=2)
    filtered = taps[0] * extended[:, :, 0:spec_dev]
    for tap_index in range(1, TAPS):
        filtered = filtered + taps[tap_index] * extended[:, :, tap_index : tap_index + spec_dev]
    filtered = filtered.astype(jnp.bfloat16).reshape(count_of_beams, 2, 2, spec_dev, chan_count)
    coarse = jnp.einsum(
        "bopsn,pnqr->boqrs", filtered, coarse_dft, preferred_element_type=jnp.float32
    )
    coarse = (
        (coarse * chan_count ** (-0.5))
        .astype(jnp.bfloat16)
        .reshape(count_of_beams, 4, busy_count, spec_dev)
    )
    arrived = lax.all_to_all(
        lax.all_to_all(coarse, "tm", split_axis=2, concat_axis=3, tiled=True),
        "chan",
        split_axis=2,
        concat_axis=3,
        tiled=True,
    )
    ordered = arrived.reshape(count_of_beams, 4, CH_DEV, chan_devices, tm_count, spec_dev)
    ordered = ordered.transpose(0, 1, 2, 4, 3, 5).reshape(
        count_of_beams, 4, CH_DEV, tm_count * chan_devices * spec_dev
    )
    powers = detect_power(ordered)
    first_slot = lax.axis_index("chan") * (CH_DEV * tm_count) + lax.axis_index("tm") * CH_DEV
    drift_rates = slot_rates(lax.dynamic_slice_in_dim(slot_index, first_slot, CH_DEV), drift_low)
    drift_total = jnp.zeros((count_of_beams, CH_DEV, NDRIFT, FA * FB), jnp.float32)
    for group_index in range(tm_count):
        step_rows = powers[:, :, group_index * FSTEP : (group_index + 1) * FSTEP]
        drift_total = drift_total + to_bfloat(
            drift_rows(step_rows, group_index * FSTEP, drift_rates, 0, FA * FB, pad_width)
        )
    result = lax.all_to_all(
        (drift_total / step_count).astype(jnp.bfloat16),
        "tm",
        split_axis=3,
        concat_axis=1,
        tiled=True,
    ).astype(jnp.float32)
    return result


LANES = 128
FINE = FA * FB
SHORT = FINE // LANES
SLOTS = 32
HALO_ROWS = 8
PAD = 256
BLOCK = 256
DEPTH = 3


def short_dft(values, sign):
    count = len(values)
    if count == 1:
        return values
    even = short_dft(values[0::2], sign)
    odd = short_dft(values[1::2], sign)
    low, high = [], []
    for k in range(count // 2):
        term = odd[k]
        if k:
            flipped = pltpu.roll(term, LANES // 2, 1)
            angle = 2.0 * math.pi * k / count
            if 4 * k == count:
                term = flipped * sign
            else:
                term = term * math.cos(angle) + flipped * (sign * math.sin(angle))
        low.append(even[k] + term)
        high.append(even[k] - term)
    return low + high


def first_block(part):
    return jnp.clip(2 * part - 1, 0, (FINE - 2 * PAD) // BLOCK - 2)


def front_kernel(
    tm_count, chan_devices, volt, taps_ref, mask_ref, rate_ref, trig_hbm, dft_hbm, tap_ref, pick_ref,
    out_ref, low_ref, vbuf, halo, trig, dft, weight, edge, g00, g01, g10, g11, spec, mid, power, send, held,
    volt_sem, const_sem, halo_sem, swap_sent, swap_came, sent1, came1, sent2, came2,
):
    beams, lanes, rows, chan_count = volt.shape
    items = beams // 2
    count = rows // SHORT
    tm, chan = lax.axis_index("tm"), lax.axis_index("chan")
    core = lax.rem(chan, 2)
    place = tm * chan_devices + chan
    last_place = tm_count * chan_devices - 1
    MESH = pl.DeviceIdType.MESH
    tm_peers = [lax.rem(tm + q, tm_count) for q in range(tm_count)]
    chan_peers = [lax.rem(chan + k, chan_devices) for k in range(chan_devices)]
    chan_from = [lax.rem(chan + chan_devices - k, chan_devices) for k in range(chan_devices)]
    tm_from = [lax.rem(tm + tm_count - q, tm_count) for q in range(tm_count)]
    before = lax.rem(place + last_place, last_place + 1)
    after = lax.rem(place + 1, last_place + 1)
    before_id = (before // chan_devices, lax.rem(before, chan_devices))
    after_id = (after // chan_devices, lax.rem(after, chan_devices))

    barrier = pltpu.get_barrier_semaphore()
    for q in range(1, tm_count):
        pl.semaphore_signal(barrier, inc=1, device_id=(tm_peers[q], chan), device_id_type=MESH)
    for k in range(1, chan_devices):
        pl.semaphore_signal(barrier, inc=1, device_id=(tm, chan_peers[k]), device_id_type=MESH)
    pl.semaphore_signal(barrier, inc=1, device_id=before_id, device_id_type=MESH)
    pl.semaphore_signal(barrier, inc=1, device_id=after_id, device_id_type=MESH)

    def volt_copy(i):
        beam = lax.rem(core + 1 + i, 2) * items + i // 2
        slot = lax.rem(i, DEPTH)
        return pltpu.make_async_copy(volt.at[beam], vbuf.at[slot], volt_sem.at[slot])

    trig_copy = pltpu.make_async_copy(trig_hbm, trig, const_sem.at[0])
    dft_copy = pltpu.make_async_copy(dft_hbm, dft, const_sem.at[1])
    trig_copy.start()
    volt_copy(0).start()
    volt_copy(1).start()
    dft_copy.start()

    square = (chan_count, chan_count)
    row = lax.broadcasted_iota(jnp.int32, square, 0)
    column = lax.broadcasted_iota(jnp.int32, square, 1)
    mask = mask_ref[...].astype(jnp.float32)
    counted = jnp.where(column < row, mask, jnp.where(column == row, (1.0 - mask) * chan_count, 0.0))
    ones = jnp.ones((chan_count, 2 * LANES), jnp.bfloat16)
    order = jnp.dot(counted.astype(jnp.bfloat16), ones, preferred_element_type=jnp.float32)
    lane = lax.broadcasted_iota(jnp.int32, (chan_count, 2 * LANES), 1)
    slot_of = lax.rem(lane, SLOTS).astype(jnp.float32)
    picked = jnp.where(order == slot_of, 1.0, 0.0).astype(jnp.bfloat16)
    low_ref[...] = jnp.dot(
        jnp.broadcast_to(rate_ref[...].astype(jnp.float32), (8, chan_count)).astype(jnp.bfloat16),
        picked[:, :LANES],
        preferred_element_type=jnp.float32,
    )
    trig_copy.wait()
    cosines = jnp.dot(trig[0], picked, preferred_element_type=jnp.float32)
    sines = jnp.dot(trig[1], picked, preferred_element_type=jnp.float32)
    pl.semaphore_wait(barrier, tm_count + chan_devices)

    halo_copy = pltpu.make_async_remote_copy(
        src_ref=volt.at[:, :, pl.ds(0, HALO_ROWS), :],
        dst_ref=halo,
        send_sem=halo_sem.at[0],
        recv_sem=halo_sem.at[1],
        device_id=before_id,
        device_id_type=MESH,
    )

    @pl.when(place > 0)
    def _():
        halo_copy.start()

    imag = lax.rem(lane // 64, 2) == 1
    upper = jnp.where(imag, -sines, cosines)
    lower = jnp.where(imag, cosines, sines)
    taps = taps_ref[...] * chan_count ** (-0.5)
    taps_high = taps.astype(jnp.bfloat16)
    taps_low = (taps - taps_high.astype(jnp.float32)).astype(jnp.bfloat16)
    taps_pair = jnp.concatenate([taps_high.astype(jnp.float32), taps_low.astype(jnp.float32)], axis=0)
    taps_pair = taps_pair.T.astype(jnp.bfloat16)
    for pol in range(2):
        factor = jnp.dot(taps_pair, tap_ref[pol], preferred_element_type=jnp.float32)
        weight[pol, :chan_count] = (upper * factor).astype(jnp.bfloat16)
        weight[pol, chan_count:] = (lower * factor).astype(jnp.bfloat16)

    grams = ((g00, g01), (g10, g11))
    chunk = 256
    per_chunk = chunk // SHORT
    first_pol = lax.rem(lax.broadcasted_iota(jnp.int32, (per_chunk, LANES), 1) // SLOTS, 2) == 0
    sign_of = lambda n: jnp.where(
        lax.broadcasted_iota(jnp.int32, (n, LANES), 1) < LANES // 2, 1.0, -1.0
    ).astype(jnp.float32)

    def matmuls(slot, start):
        for pol in range(2):
            left, right = grams[pol]
            part = jnp.dot(
                jnp.concatenate(
                    [vbuf[slot, 2 * pol, start : start + chunk], vbuf[slot, 2 * pol + 1, start : start + chunk]],
                    axis=1,
                ),
                weight[pol],
                preferred_element_type=jnp.float32,
            )
            left[start : start + chunk] = part[:, :LANES]
            right[start : start + chunk] = part[:, LANES:]

    def combine(i, start):
        def both(at):
            low = pl.ds(start + at, per_chunk, stride=SHORT)
            high = pl.ds(start + at + 2, per_chunk, stride=SHORT)
            return g00[low, :] + g01[high, :], g10[low, :] + g11[high, :]

        here = both(0)
        where = pl.ds(pl.multiple_of(core * count + start // SHORT, per_chunk), per_chunk)
        for at in range(SHORT):
            later = both(at + 1)
            value = jnp.where(
                first_pol,
                here[0] + pltpu.roll(later[0], LANES - SLOTS, 1),
                here[1] + pltpu.roll(later[1], SLOTS, 1),
            )
            spec[i, at, where, :] = value.astype(jnp.bfloat16)
            here = later

    def swap(i):
        half = pl.ds(pl.multiple_of(core * count, count), count)
        return pltpu.make_async_remote_copy(
            src_ref=spec.at[i, :, half, :],
            dst_ref=spec.at[i + 1, :, half, :],
            send_sem=swap_sent.at[i // 2],
            recv_sem=swap_came.at[i // 2],
            device_id=(tm, chan + 1 - 2 * core),
            device_id_type=MESH,
        )

    def fine(i, item):
        sign_full = sign_of(LANES)
        for at in range(SHORT):
            plain = spec[i, at]
            flipped = (pltpu.roll(plain.astype(jnp.float32), LANES // 2, 1) * sign_full).astype(jnp.bfloat16)
            mid[at] = jnp.dot(
                dft[at], jnp.concatenate([plain, flipped], axis=0), preferred_element_type=jnp.float32
            )
        step = 16
        sign = sign_of(step)

        @pl.loop(0, LANES // step)
        def _(block):
            at_row = pl.multiple_of(block * step, step)
            spectra = short_dft([mid[at, pl.ds(at_row, step), :] for at in range(SHORT)], sign)
            for high, value in enumerate(spectra):
                where = pl.ds(pl.multiple_of(high // 2 * LANES + at_row, step), step)
                power[where, high % 2 * LANES : (high % 2 + 1) * LANES] = (value * value).astype(jnp.bfloat16)

        for pair in range(FINE // BLOCK // 2):
            sums = lax.dot_general(
                pick_ref[...],
                power[pair * BLOCK : (pair + 1) * BLOCK, :],
                (((1,), (1,)), ((), ())),
                preferred_element_type=jnp.float32,
            )
            for group in range(chan_devices):
                for side in range(2):
                    send[item, group, 2 * pair + side] = sums[
                        group * 8 : group * 8 + 8, side * LANES : (side + 1) * LANES
                    ].astype(jnp.bfloat16)

    def along_chan(item, k):
        return pltpu.make_async_remote_copy(
            src_ref=send.at[item, chan_peers[k]],
            dst_ref=held.at[item, k],
            send_sem=sent1.at[item, k],
            recv_sem=came1.at[item, k],
            device_id=(tm, chan_peers[k]),
            device_id_type=MESH,
        )

    def along_tm(item, k, q):
        block = held.at[item, k] if k else send.at[item, chan]
        return pltpu.make_async_remote_copy(
            src_ref=block.at[pl.ds(first_block(tm_peers[q]), 4)],
            dst_ref=out_ref.at[tm, chan_from[k], item],
            send_sem=sent2.at[item, k, q],
            recv_sem=came2.at[item, k, q],
            device_id=(tm_peers[q], chan),
            device_id_type=MESH,
        )

    def forward(item):
        for k in range(chan_devices):
            if k:
                along_chan(item, k).wait_recv()
            for q in range(1, tm_count):
                along_tm(item, k, q).start()
            near = pl.ds(first_block(tm), 4)
            out_ref[tm, chan_from[k], item] = held[item, k, near] if k else send[item, chan, near]

    @pl.loop(0, beams)
    def _(i):
        slot = lax.rem(i, DEPTH)
        item = i // 2
        beam = lax.rem(core + 1 + i, 2) * items + item
        volt_copy(i).wait()

        @pl.when(i + 2 < beams)
        def _():
            volt_copy(i + 2).start()

        for start in range(0, rows, chunk):
            matmuls(slot, start)
            if start:
                combine(i, start - chunk)

        @pl.when(i == 0)
        def _():
            @pl.when(place < last_place)
            def _():
                halo_copy.wait_recv()

            @pl.when(place == last_place)
            def _():
                halo[...] = jnp.zeros_like(halo)

            for pol in range(2):
                part = jnp.dot(
                    jnp.concatenate(
                        [
                            halo[:, 2 * pol].reshape(beams * HALO_ROWS, chan_count),
                            halo[:, 2 * pol + 1].reshape(beams * HALO_ROWS, chan_count),
                        ],
                        axis=1,
                    ),
                    weight[pol],
                    preferred_element_type=jnp.float32,
                )
                edge[pol] = part

        here = pl.ds(pl.multiple_of(beam * HALO_ROWS, HALO_ROWS), HALO_ROWS)
        for pol in range(2):
            left, right = grams[pol]
            left[rows : rows + HALO_ROWS] = edge[pol, here, :LANES]
            right[rows : rows + HALO_ROWS] = edge[pol, here, LANES:]
        combine(i, rows - chunk)

        @pl.when(lax.rem(i, 2) == 0)
        def _():
            swap(i).start()

        @pl.when(lax.rem(i, 2) == 1)
        def _():
            @pl.when(i == 1)
            def _():
                dft_copy.wait()

            swap(i - 1).wait_recv()
            fine(i, item)
            for k in range(1, chan_devices):
                along_chan(item, k).start()

            @pl.when(item > 0)
            def _():
                forward(item - 1)

    forward(items - 1)

    @pl.when(place > 0)
    def _():
        halo_copy.wait_send()

    @pl.loop(0, items)
    def _(item):
        swap(2 * item).wait_send()
        for k in range(chan_devices):
            if k:
                along_chan(item, k).wait_send()
            for q in range(1, tm_count):
                along_tm(item, k, q).wait_send()
        for k in range(chan_devices):
            for q in range(1, tm_count):
                pltpu.make_async_remote_copy(
                    src_ref=held.at[item, k, pl.ds(0, 4)],
                    dst_ref=out_ref.at[tm_from[q], chan_from[k], item],
                    send_sem=sent2.at[item, k, q],
                    recv_sem=came2.at[item, k, q],
                    device_id=(tm_peers[q], chan),
                    device_id_type=MESH,
                ).wait_recv()


def front(voltages, taps, busy_mask, drift_low, tm_count, chan_devices):
    beams, lanes, rows, chan_count = voltages.shape
    items = beams // 2
    ids = np.arange(chan_count)
    angles = (ids[:, None] * ids[None, :] % chan_count) * (2.0 * math.pi / chan_count)
    trig = jnp.asarray(np.stack([np.cos(angles), np.sin(angles)]), jnp.bfloat16)
    position = np.arange(SHORT)[:, None, None] + SHORT * np.arange(LANES)[None, None, :]
    turns = (position * np.arange(LANES)[None, :, None] % FINE) * (2.0 * math.pi / FINE)
    dft = jnp.asarray(np.concatenate([np.cos(turns), np.sin(turns)], axis=2), jnp.bfloat16)
    column = np.arange(2 * LANES)
    tap_of = np.stack([2 * (column // LANES) + (column // SLOTS % 2 ^ pol) for pol in range(2)])
    tap_pick = tap_of[:, None, :] == (np.arange(2 * TAPS) % TAPS)[None, :, None]
    per_group = SLOTS // chan_devices
    line = np.arange(8 * chan_devices)
    group, side, slot = line // 8, line % 8 // per_group, line % per_group
    lane = np.arange(2 * LANES)
    pick = (side[:, None] == lane[None, :] // LANES) & (
        (group * per_group + slot)[:, None] == lane[None, :] % SLOTS
    )
    vmem = pl.BlockSpec(memory_space=pltpu.VMEM)
    hbm = pl.BlockSpec(memory_space=pl.ANY)
    dma = pltpu.SemaphoreType.DMA
    kernel = lambda *refs: front_kernel(tm_count, chan_devices, *refs)
    blocks = FINE // BLOCK
    gram = pltpu.VMEM((rows + 3 * HALO_ROWS, LANES), jnp.float32)
    return pl.pallas_call(
        kernel,
        in_specs=[hbm, vmem, vmem, vmem, hbm, hbm, vmem, vmem],
        out_specs=(vmem, vmem),
        out_shape=(
            jax.ShapeDtypeStruct((tm_count, chan_devices, items, 4, 8, LANES), jnp.bfloat16),
            jax.ShapeDtypeStruct((8, LANES), jnp.float32),
        ),
        scratch_shapes=[
            pltpu.VMEM((DEPTH, lanes, rows, chan_count), jnp.bfloat16),
            pltpu.VMEM((beams, lanes, HALO_ROWS, chan_count), jnp.bfloat16),
            pltpu.VMEM(trig.shape, jnp.bfloat16),
            pltpu.VMEM(dft.shape, jnp.bfloat16),
            pltpu.VMEM((2, 2 * chan_count, 2 * LANES), jnp.bfloat16),
            pltpu.VMEM((2, beams * HALO_ROWS, 2 * LANES), jnp.float32),
            gram,
            gram,
            gram,
            gram,
            pltpu.VMEM((beams, SHORT, LANES, LANES), jnp.bfloat16),
            pltpu.VMEM((SHORT, LANES, LANES), jnp.float32),
            pltpu.VMEM((FINE // 2, 2 * LANES), jnp.bfloat16),
            pltpu.VMEM((items, chan_devices, blocks, 8, LANES), jnp.bfloat16),
            pltpu.VMEM((items, chan_devices, blocks, 8, LANES), jnp.bfloat16),
            dma((DEPTH,)),
            dma((2,)),
            dma((2,)),
            dma((items,)),
            dma((items,)),
            dma((items, chan_devices)),
            dma((items, chan_devices)),
            dma((items, chan_devices, tm_count)),
            dma((items, chan_devices, tm_count)),
        ],
        compiler_params=pltpu.CompilerParams(
            collective_id=0, has_side_effects=True, vmem_limit_bytes=56 * 2**20
        ),
    )(
        voltages,
        taps,
        busy_mask.reshape(1, chan_count),
        drift_low.reshape(1, chan_count),
        trig,
        dft,
        jnp.asarray(tap_pick, jnp.bfloat16),
        jnp.asarray(pick, jnp.bfloat16),
    )


STRIDE = 40


def drift_kernel(scale, place_ref, low_ref, in_ref, out_ref, rows_ref, stage_ref):
    steps, beams, tiles, _, _ = in_ref.shape
    _, _, rates, width = out_ref.shape
    slots = rows_ref.shape[0]
    pad = PAD // LANES
    wide = 2 * tiles
    out_tiles = width // LANES
    slot = pl.program_id(0)

    @pl.when(slot == 0)
    def _():
        empty = jnp.zeros((beams, LANES), jnp.float32)

        @pl.loop(0, steps)
        def _(t):
            for beam in range(beams):
                stage_ref[beam * STRIDE : beam * STRIDE + 8 * tiles] = (
                    in_ref[t, beam].astype(jnp.float32).reshape(8 * tiles, LANES)
                )
            for at in range(slots):
                for tile in range(pad):
                    rows_ref[at, t, tile] = empty
                    rows_ref[at, t, pad + wide + tile] = empty
                for tile in range(wide):
                    rows_ref[at, t, pad + tile] = stage_ref[pl.ds(tile * slots + at, beams, stride=STRIDE), :]

    lane8 = lax.broadcasted_iota(jnp.int32, (8, LANES), 1)
    low = jnp.sum(jnp.where(lane8 == place_ref[0] + slot, low_ref[...], 0.0)[:1]).astype(jnp.int32)
    lane = lax.broadcasted_iota(jnp.int32, (beams, LANES), 1)
    origin = place_ref[1] + PAD
    for rate in range(rates):
        totals = None
        for t in range(steps):
            start = (low * t + origin) + rate * t
            base = lax.shift_right_logical(start, 7)
            rest = start & (LANES - 1)
            parts = rows_ref[slot, t, pl.ds(base, out_tiles + (t > 0))]
            if t:
                keep = lane >= rest
                back = (LANES - rest) & (LANES - 1)
                parts = [
                    pltpu.roll(jnp.where(keep, parts[k], parts[k + 1]), back, 1) for k in range(out_tiles)
                ]
                totals = [total + part for total, part in zip(totals, parts)]
            else:
                totals = [parts[k] for k in range(out_tiles)]
        out_ref[:, 0, rate, :] = jnp.concatenate(totals, axis=1) * scale


def drift_sums(arrived, low_rates, place, slots, width):
    steps, beams, tiles, _, _ = arrived.shape
    kernel = lambda *refs: drift_kernel(1.0 / (4.0 * FINE * steps), *refs)
    vmem = pl.BlockSpec(memory_space=pltpu.VMEM)
    return pl.pallas_call(
        kernel,
        grid=(slots,),
        in_specs=[pl.BlockSpec(memory_space=pltpu.SMEM), vmem, vmem],
        out_specs=pl.BlockSpec((beams, 1, NDRIFT, width), lambda s: (0, s, 0, 0)),
        out_shape=jax.ShapeDtypeStruct((beams, slots, NDRIFT, width), jnp.float32),
        scratch_shapes=[
            pltpu.VMEM((slots, steps, 2 * tiles + 2 * PAD // LANES + 1, beams, LANES), jnp.float32),
            pltpu.VMEM((beams * STRIDE, LANES), jnp.float32),
        ],
        compiler_params=pltpu.CompilerParams(vmem_limit_bytes=48 * 2**20),
    )(place, low_rates, arrived)


def paired_shards(voltages, taps, busy_mask, drift_low):
    tm_count = lax.axis_size("tm")
    chan_devices = lax.axis_size("chan")
    beams = voltages.shape[0]
    slots = SLOTS // chan_devices
    arrived, low_rates = front(voltages, taps, busy_mask, drift_low, tm_count, chan_devices)
    arrived = arrived.reshape(tm_count * chan_devices // 2, beams, 4, 8, LANES)
    tm, chan = lax.axis_index("tm"), lax.axis_index("chan")
    width = FINE // tm_count
    place = jnp.stack([chan * slots, tm * width - BLOCK * first_block(tm)])
    return drift_sums(arrived, low_rates, place, slots, width)


def two_devices_hold_a_step(mesh, voltages):
    tm_count, chan_devices = mesh.shape["tm"], mesh.shape["chan"]
    rows = voltages.shape[2] // (tm_count * chan_devices)
    return (
        2 * rows == FINE
        and tm_count == 4
        and chan_devices == 2 * FSTEP
        and CH_DEV * tm_count * chan_devices == SLOTS
        and voltages.shape[0] == 8
        and PAD >= DSPAN * (FSTEP * tm_count - 1)
    )


def solution(mesh):
    in_specs = (P(None, None, ("tm", "chan"), None), P(), P(), P())
    out_specs = P(None, "chan", None, "tm")

    def run(voltages, taps, busy_mask, drift_low):
        body = paired_shards if two_devices_hold_a_step(mesh, voltages) else shards
        return jax.shard_map(
            body, mesh=mesh, in_specs=in_specs, out_specs=out_specs, check_vma=False
        )(voltages, taps, busy_mask, drift_low)

    return run
```

time: 80.2 us -> 59.2 us (0.74)
  Pallas kernels: 67 us -> 56.9 us
  starting transfers between devices: 3.43 us -> 0 us
  matrix products: 3.13 us -> 0 us
  other arithmetic: 2.9 us -> 0.07 us
  local copies, waits for them, and re-layouts: 3.1 us -> 1.9 us
    pallas_call x5 -> x2, Pallas kernels: 67 us -> 56.9 us  [the longest x1 50 us: front(): pl.pallas_call(kernel, in_specs=[hbm, vmem, vmem, vmem, hbm, hbm, vmem, v...]
    ppermute x2 -> x0, starting transfers between devices: 3.43 us -> none  [the longest x1 2.14 us: paired_shards(): lax.ppermute(sent, 'chan', [(i, i ^ 1) for i in range(chan_devices)])]
    dot_general x2 -> x0, matrix products: 3.13 us -> none  [the longest x1 1.65 us: tap_weights(): cosines = jnp.dot(cos_table, picked, preferred_element_type=jnp.float32)]
    reduce_sum x2 -> x0, other arithmetic: 1.28 us -> none  [the longest x1 1.16 us: tap_weights(): before = jnp.sum(jnp.where(earlier, busy_mask[None, :], 0), axis=1)]
    slice x2 -> x0, local copies, waits for them, and re-layouts: 1 us -> none  [the longest x1 0.99 us: paired_shards(): halo = passed_along(voltages[:, :, :HALO_ROWS], ('tm', 'chan'), -1)]
    unnamed x12 -> x4, local copies, waits for them, and re-layouts: 2.02 us -> 1.9 us
  transfers between devices with their start and end apart: 2 -> 0, of which waited for: 0 -> 0; matrix products, arithmetic and copies ran while one was open for 8% -> 0% of each run, Pallas kernels for 12% -> 0%
where the time goes in v1:
time: 59.2 us; the launch traced here: 58.9 us
  Pallas kernels  56.9 us (96%)
  local copies, waits for them, and re-layouts  1.9 us (3%)
    pallas_call x1, Pallas kernels, front(): pl.pallas_call(kernel, in_specs=[hbm, vmem, vmem, vmem, hbm, hbm, vmem, v...  50 us
    pallas_call x1, Pallas kernels, drift_sums(): pl.pallas_call(kernel, grid=(slots,), in_specs=[pl.BlockSpec(memory_space...  6.96 us
    unnamed x4, local copies, waits for them, and re-layouts  1.9 us

profile of v1, /device:TPU:0, one launch (start us, length us, event | category | flops | bytes accessed | tf_op | source)
XLA Modules:
  0.0 58.9 jit_solution(2200169076579203992)
XLA Ops:
  0.0 0.1 pad_add_fusion.refs_0_
  0.1 50.0 %shard_map.82 = (bf16[4,8,4,4,8,128]{5,4,3,2,1,0:T(8,128)(2,1)}, f32[8,128]{1,0:T(8,128)}) custom-call(bf16[8,4,1024,512]{3,2,1,0:T(8,128)(2,1)} %refs_0_.1, f32[4,512]{1,0:T(4,128)} %refs_1_.1, s32[1,512]{1,0:T(1,128)} %bitcast.6, s32[1,512]{1,0:T(1,128)} %bitcast.7, bf16[2,512,512]{2,1,0:T(8,128)(2,1)} %constant.29.clone.refs_4_, ...), custom_call_target="tpu_custom_call" | custom-call | tf_op jit(solution)/shard_map/pallas_call | solution.py:515
  50.0 0.0 copy-start
  50.1 1.2 %copy-done = bf16[4,8,4,4,8,128]{5,4,3,2,1,0:T(8,128)(2,1)S(1)} copy-done((bf16[4,8,4,4,8,128]{5,4,3,2,1,0:T(8,128)(2,1)S(1)}, bf16[4,8,4,4,8,128]{5,4,3,2,1,0:T(8,128)(2,1)}, u32[]{:S(2)}) %copy-start) | copy-done | bytes 1048600
  51.3 0.0 copy-start.1
  51.3 0.7 %copy-done.1 = f32[8,128]{1,0:T(8,128)S(1)} copy-done((f32[8,128]{1,0:T(8,128)S(1)}, f32[8,128]{1,0:T(8,128)}, u32[]{:S(2)}) %copy-start.1) | copy-done | bytes 4120
  51.9 7.0 %shard_map.83 = f32[8,4,16,512]{3,2,1,0:T(8,128)} custom-call(s32[2]{0:T(128)S(1)} %pad_add_fusion.refs_0_, f32[8,128]{1,0:T(8,128)S(1)} %copy-done.1, bf16[16,8,4,8,128]{4,3,2,1,0:T(8,128)(2,1)S(1)} %bitcast.5), custom_call_target="tpu_custom_call" | custom-call | tf_op jit(solution)/shard_map/pallas_call | solution.py:620
Async XLA Ops:
  50.0 1.2 %copy-start = (bf16[4,8,4,4,8,128]{5,4,3,2,1,0:T(8,128)(2,1)S(1)}, bf16[4,8,4,4,8,128]{5,4,3,2,1,0:T(8,128)(2,1)}, u32[]{:S(2)}) copy-start(bf16[4,8,4,4,8,128]{5,4,3,2,1,0:T(8,128)(2,1)} %get-tuple-element.8) | copy-start | bytes 3145732
  51.3 0.7 %copy-start.1 = (f32[8,128]{1,0:T(8,128)S(1)}, f32[8,128]{1,0:T(8,128)}, u32[]{:S(2)}) copy-start(f32[8,128]{1,0:T(8,128)} %get-tuple-element.7.refs_1_) | copy-start | bytes 12292
